TPU v7x, 128 devices: a whole 4x4x4 slice. The times are simulated.
128 devices in a mesh: tp: 4 (over x), dp: 32 (over z, y, core).
Axes of the slice: x: 4, y: 4, z: 4, core: 2. Of those that a mesh axis runs over, the one named last changes fastest.
Arguments:
- hidden: bfloat16 [32, 256, 7168], P('dp', 'tp')
- norm_gain: bfloat16 [7168], P('dp')
- w_query: bfloat16 [7168, 7168], P('dp', 'tp')
- w_key: bfloat16 [7168, 1024], P('dp', 'tp')
- w_value: bfloat16 [7168, 1024], P('dp', 'tp')
- w_out: bfloat16 [7168, 7168], P('tp', 'dp')
- grad_out: bfloat16 [32, 256, 7168], P('dp', 'tp')
Outputs:
- output 1: bfloat16 [32, 256, 7168], P('dp', 'tp')
- output 2: bfloat16 [32, 256, 7168], P('dp', 'tp')
- output 3: float32 [7168], P('dp')
- output 4: float32 [7168, 7168], P('dp', 'tp')
- output 5: float32 [7168, 1024], P('dp', 'tp')
- output 6: float32 [7168, 1024], P('dp', 'tp')
- output 7: float32 [7168, 7168], P('tp', 'dp')
All inputs are finite; a program needn't handle non-finite values.
Results may differ from a plain program's by a relative error of at most 0.0184718.
Values are sent between devices in bfloat16 or wider.
A program may use at most 1 GiB of HBM per device.

v0:
```python
import jax
import jax.numpy as jnp
from jax import lax
from jax.sharding import PartitionSpec as P, NamedSharding

HEAD_DIM = 128
NORM_EPS = 1e-5
ROPE_BASE = 500000.0
SCORE_SCALE = HEAD_DIM ** -0.5
MASK_VALUE = -1e30


def rope_tables(seq_len):
    half_dim = HEAD_DIM // 2
    inv_freq = ROPE_BASE ** (-jnp.arange(half_dim, dtype=jnp.float32) * 2.0 / HEAD_DIM)
    angles = jnp.arange(seq_len, dtype=jnp.float32)[:, None] * inv_freq[None, :]
    return jnp.cos(angles), jnp.sin(angles)


def rotate(values, cos_t, sin_t):
    half_dim = values.shape[-1] // 2
    lower_half = values[..., :half_dim]
    upper_half = values[..., half_dim:]
    return jnp.concatenate([lower_half * cos_t - upper_half * sin_t, upper_half * cos_t + lower_half * sin_t], axis=-1)


def solution(mesh):
    def local_block(hidden, norm_gain, w_query, w_key, w_value, w_out, grad_out):
        gain_full = lax.all_gather(norm_gain, "dp", axis=0, tiled=True).astype(jnp.float32)
        wq_full = lax.all_gather(w_query, "dp", axis=0, tiled=True)
        wk_full = lax.all_gather(w_key, "dp", axis=0, tiled=True)
        wv_full = lax.all_gather(w_value, "dp", axis=0, tiled=True)
        wo_full = lax.all_gather(w_out, "dp", axis=1, tiled=True)
        batch_loc = hidden.shape[0]
        kv_loc = wk_full.shape[1] // HEAD_DIM
        group_size = wq_full.shape[1] // wk_full.shape[1]

        hidden_f32 = hidden.astype(jnp.float32)
        inv_rms = lax.rsqrt(jnp.mean(hidden_f32 * hidden_f32, axis=-1, keepdims=True) + NORM_EPS)
        x_hat = hidden_f32 * inv_rms
        normed = lax.all_gather((x_hat * gain_full).astype(jnp.bfloat16), "tp", axis=1, tiled=True)
        seq_len = normed.shape[1]
        q_shape = (batch_loc, seq_len, kv_loc, group_size, HEAD_DIM)
        k_shape = (batch_loc, seq_len, kv_loc, HEAD_DIM)
        cos_t, sin_t = rope_tables(seq_len)
        cos_q, sin_q = cos_t[:, None, None, :], sin_t[:, None, None, :]
        cos_k, sin_k = cos_t[:, None, :], sin_t[:, None, :]

        q_lin = jnp.einsum("bsd,de->bse", normed, wq_full, preferred_element_type=jnp.float32).astype(jnp.bfloat16)
        k_lin = jnp.einsum("bsd,de->bse", normed, wk_full, preferred_element_type=jnp.float32).astype(jnp.bfloat16)
        v_heads = jnp.einsum("bsd,de->bse", normed, wv_full, preferred_element_type=jnp.float32).astype(jnp.bfloat16).reshape(k_shape)
        q_heads = rotate(q_lin.reshape(q_shape).astype(jnp.float32), cos_q, sin_q).astype(jnp.bfloat16)
        k_heads = rotate(k_lin.reshape(k_shape).astype(jnp.float32), cos_k, sin_k).astype(jnp.bfloat16)

        causal = jnp.arange(seq_len)[:, None] >= jnp.arange(seq_len)[None, :]
        scores = jnp.einsum("bqgrd,bkgd->bgrqk", q_heads, k_heads, preferred_element_type=jnp.float32) * SCORE_SCALE
        attn_prob = jax.nn.softmax(jnp.where(causal, scores, MASK_VALUE), axis=-1)
        prob_bf16 = attn_prob.astype(jnp.bfloat16)
        attn_out = jnp.einsum("bgrqk,bkgd->bqgrd", prob_bf16, v_heads, preferred_element_type=jnp.float32).astype(jnp.bfloat16).reshape(batch_loc, seq_len, -1)
        out_part = jnp.einsum("bse,ed->bsd", attn_out, wo_full, preferred_element_type=jnp.float32).astype(jnp.bfloat16)
        out_loc = lax.psum_scatter(out_part, "tp", scatter_dimension=1, tiled=True)
        hidden_out = (hidden_f32 + out_loc.astype(jnp.float32)).astype(jnp.bfloat16)

        grad_full = lax.all_gather(grad_out, "tp", axis=1, tiled=True)
        grad_wo = jnp.einsum("bse,bsd->ed", attn_out, grad_full, preferred_element_type=jnp.float32)
        grad_attn = jnp.einsum("bsd,ed->bse", grad_full, wo_full, preferred_element_type=jnp.float32).astype(jnp.bfloat16).reshape(q_shape)
        grad_v = jnp.einsum("bgrqk,bqgrd->bkgd", prob_bf16, grad_attn, preferred_element_type=jnp.float32).astype(jnp.bfloat16)
        grad_prob = jnp.einsum("bqgrd,bkgd->bgrqk", grad_attn, v_heads, preferred_element_type=jnp.float32).astype(jnp.bfloat16).astype(jnp.float32)
        grad_scores = attn_prob * (grad_prob - jnp.sum(grad_prob * attn_prob, axis=-1, keepdims=True))
        grad_scores = (grad_scores * SCORE_SCALE).astype(jnp.bfloat16)
        grad_q = jnp.einsum("bgrqk,bkgd->bqgrd", grad_scores, k_heads, preferred_element_type=jnp.float32).astype(jnp.bfloat16)
        grad_k = jnp.einsum("bgrqk,bqgrd->bkgd", grad_scores, q_heads, preferred_element_type=jnp.float32).astype(jnp.bfloat16)
        grad_q_lin = rotate(grad_q.astype(jnp.float32), cos_q, -sin_q).astype(jnp.bfloat16).reshape(batch_loc, seq_len, -1)
        grad_k_lin = rotate(grad_k.astype(jnp.float32), cos_k, -sin_k).astype(jnp.bfloat16).reshape(batch_loc, seq_len, -1)
        grad_v_lin = grad_v.reshape(batch_loc, seq_len, -1)
        grad_normed_part = (
            jnp.einsum("bse,de->bsd", grad_q_lin, wq_full, preferred_element_type=jnp.float32)
            + jnp.einsum("bse,de->bsd", grad_k_lin, wk_full, preferred_element_type=jnp.float32)
            + jnp.einsum("bse,de->bsd", grad_v_lin, wv_full, preferred_element_type=jnp.float32)
        ).astype(jnp.bfloat16)
        grad_normed = lax.psum_scatter(grad_normed_part, "tp", scatter_dimension=1, tiled=True).astype(jnp.float32)
        grad_wq = jnp.einsum("bsd,bse->de", normed, grad_q_lin, preferred_element_type=jnp.float32)
        grad_wk = jnp.einsum("bsd,bse->de", normed, grad_k_lin, preferred_element_type=jnp.float32)
        grad_wv = jnp.einsum("bsd,bse->de", normed, grad_v_lin, preferred_element_type=jnp.float32)
        gain_part = jnp.sum(grad_normed * x_hat, axis=(0, 1))
        grad_gain = lax.psum(lax.psum_scatter(gain_part, "dp", scatter_dimension=0, tiled=True), "tp")
        value_a9 = grad_normed * gain_full
        grad_hidden = (grad_out.astype(jnp.float32) + inv_rms * (value_a9 - x_hat * jnp.mean(value_a9 * x_hat, axis=-1, keepdims=True))).astype(jnp.bfloat16)
        return (
            hidden_out,
            grad_hidden,
            grad_gain,
            lax.psum_scatter(grad_wq, "dp", scatter_dimension=0, tiled=True),
            lax.psum_scatter(grad_wk, "dp", scatter_dimension=0, tiled=True),
            lax.psum_scatter(grad_wv, "dp", scatter_dimension=0, tiled=True),
            lax.psum_scatter(grad_wo, "dp", scatter_dimension=1, tiled=True),
        )

    act_spec = P("dp", "tp", None)
    col_spec = P("dp", "tp")
    row_spec = P("tp", "dp")
    return jax.shard_map(
        local_block,
        mesh=mesh,
        in_specs=(act_spec, P("dp"), col_spec, col_spec, col_spec, row_spec, act_spec),
        out_specs=(act_spec, act_spec, P("dp"), col_spec, col_spec, col_spec, row_spec),
        check_vma=False,
    )
```

profile of v0, /device:TPU:1, one launch (start us, length us, event | category | flops | bytes accessed | tf_op | source)
XLA Modules:
  0.0 1297.6 jit_solution(16026213986750747797)
XLA Ops:
  11.6 125.6 %all-reduce = bf16[7168]{0:T(1024)(128)(2,1)S(1)} all-reduce(bf16[7168]{0:T(1024)(128)(2,1)S(1)} %dynamic-update-slice), channel_id=1, replica_groups=mesh['tp'=4,'dp'=32] {'dp'}, use_global_device_ids=true, to_apply=%add | all-reduce | flops 7168 | bytes 28672
  144.0 40.9 %all-gather.7.cloned.1.call-done = bf16[1,256,7168]{2,1,0:T(8,128)(2,1)} async-done(((bf16[1,64,7168]{2,1,0:T(8,128)(2,1)}), bf16[1,256,7168]{2,1,0:T(8,128)(2,1)}) %all-gather.7.cloned.1.call-update) | async-done | bytes 3670032 | tf_op jit(solution)/shard_map/all_gather | solution.py:41
  184.9 48.8 %all-gather.11.cloned.1.call-done = bf16[7168,256]{1,0:T(8,128)(2,1)} async-done(((bf16[224,256]{1,0:T(8,128)(2,1)}), bf16[7168,256]{1,0:T(8,128)(2,1)}) %all-gather.11.cloned.1.call-update) | async-done | bytes 3670032 | tf_op jit(solution)/shard_map/all_gather | solution.py:31
  233.7 4.7 fusion.70
  238.8 42.0 %all-gather.9.cloned.1.call-done = bf16[7168,256]{1,0:T(8,128)(2,1)} async-done(((bf16[224,256]{1,0:T(8,128)(2,1)}), bf16[7168,256]{1,0:T(8,128)(2,1)}) %all-gather.9.cloned.1.call-update) | async-done | bytes 3670032 | tf_op jit(solution)/shard_map/all_gather | solution.py:32
  280.8 5.3 fusion.67
  286.1 38.4 %all-gather.17.cloned.1.call-done = bf16[1,256,7168]{2,1,0:T(8,128)(2,1)} async-done(((bf16[1,64,7168]{2,1,0:T(8,128)(2,1)}), bf16[1,256,7168]{2,1,0:T(8,128)(2,1)}) %all-gather.17.cloned.1.call-update) | async-done | bytes 3670032 | tf_op jit(solution)/shard_map/all_gather | solution.py:64
  324.5 96.4 %all-gather.15.cloned.1.call-done = bf16[1792,7168]{0,1:T(8,128)(2,1)} async-done(((bf16[1792,224]{0,1:T(8,128)(2,1)}), bf16[1792,7168]{0,1:T(8,128)(2,1)}) %all-gather.15.cloned.1.call-update) | async-done | bytes 25690128 | tf_op jit(solution)/shard_map/all_gather | solution.py:33
  420.9 13.0 fusion.38
  435.2 80.4 %all-gather.13.cloned.1.call-done = bf16[7168,1792]{1,0:T(8,128)(2,1)} async-done(((bf16[224,1792]{1,0:T(8,128)(2,1)}), bf16[7168,1792]{1,0:T(8,128)(2,1)}) %all-gather.13.cloned.1.call-update) | async-done | bytes 25690128 | tf_op jit(solution)/shard_map/all_gather | solution.py:30
  515.6 14.1 %fusion.35 = f32[256,1792]{1,0:T(8,128)} fusion(bf16[7168,1792]{1,0:T(8,128)(2,1)} %all-gather.13.cloned.1.call-done, bf16[1,256,7168]{2,1,0:T(8,128)(2,1)} %all-gather.7.cloned.1.call-done), kind=kOutput, calls=%fused_computation.42 | convolution fusion | flops 6577586176 | bytes 31195136 | tf_op jit(solution)/shard_map/bsd,de->bse/dot_general | solution.py:49
  548.1 13.9 %fusion.92 = f32[256,7168]{1,0:T(8,128)} fusion(bf16[256,1792]{0,1:T(8,128)(2,1)S(1)} %bitcast.186, bf16[7168,1792]{1,0:T(8,128)(2,1)} %all-gather.13.cloned.1.call-done), kind=kOutput, calls=%fused_computation.105 | convolution fusion | flops 6576668672 | bytes 33947648 | tf_op jit(solution)/shard_map/bse,de->bsd/dot_general | solution.py:77
  562.0 5.5 convolution_add_fusion.1
  574.6 13.1 %fusion.2 = bf16[1,256,7168]{2,1,0:T(8,128)(2,1)} fusion(bf16[256,1792]{0,1:T(8,128)(2,1)S(1)} %bitcast.191, bf16[1792,7168]{0,1:T(8,128)(2,1)} %all-gather.15.cloned.1.call-done), kind=kOutput, calls=%fused_computation.5 | convolution fusion | flops 6578503680 | bytes 30277632 | tf_op jit(solution)/shard_map/bse,ed->bsd/dot_general | solution.py:60
  587.8 6.1 fusion.13
  594.2 6.2 fusion.15
  600.5 22.4 %fusion.17 = f32[7168,1792]{1,0:T(8,128)} fusion(bf16[256,1792]{0,1:T(8,128)(2,1)S(1)} %bitcast.187, bf16[1,256,7168]{2,1,0:T(8,128)(2,1)} %all-gather.7.cloned.1.call-done), kind=kOutput, calls=%fused_computation.22 | convolution fusion | flops 6576668672 | bytes 55967744 | tf_op jit(solution)/shard_map/bsd,bse->de/dot_general | solution.py:82
  623.0 21.3 %fusion.9 = f32[1792,7168]{0,1:T(8,128)} fusion(bf16[256,1792]{0,1:T(8,128)(2,1)S(1)} %bitcast.192, bf16[1,256,7168]{2,1,0:T(8,128)(2,1)} %all-gather.17.cloned.1.call-done), kind=kOutput, calls=%fused_computation.14 | convolution fusion | flops 6576668672 | bytes 55967744 | tf_op jit(solution)/shard_map/bse,bsd->ed/dot_general | solution.py:65
  647.3 121.5 %all-reduce.1 = f32[7168]{0:T(1024)S(1)} all-reduce(f32[7168]{0:T(1024)S(1)} %get-tuple-element.7), channel_id=4, replica_groups=mesh['tp'=4,'dp'=32] {'dp'}, use_global_device_ids=true, to_apply=%region_8.9.clone | all-reduce | flops 7168 | bytes 57344
  768.9 9.2 psum.7
  778.1 3.4 fusion.44
  781.5 58.5 %reduce-scatter.13.cloned.1.call-done = f32[224,256]{1,0:T(8,128)} async-done(((f32[7168,256]{1,0:T(8,128)}), f32[224,256]{1,0:T(8,128)}) %reduce-scatter.13.cloned.1.call-update) | async-done | bytes 229392 | tf_op jit(solution)/shard_map/reduce_scatter | solution.py:94
  840.0 225.8 %reduce-scatter.11.cloned.1.call-done = f32[224,1792]{1,0:T(8,128)} async-done(((f32[7168,1792]{1,0:T(8,128)}), f32[224,1792]{1,0:T(8,128)}) %reduce-scatter.11.cloned.1.call-update) | async-done | bytes 1605648 | tf_op jit(solution)/shard_map/reduce_scatter | solution.py:93
  1065.8 224.5 %reduce-scatter.17.cloned.1.call-done = f32[1792,224]{0,1:T(8,128)} async-done(((f32[1792,7168]{0,1:T(8,128)}), f32[1792,224]{0,1:T(8,128)}) %reduce-scatter.17.cloned.1.call-update) | async-done | bytes 1605648 | tf_op jit(solution)/shard_map/reduce_scatter | solution.py:96
  (87 shorter events, 40.2 us)
Async XLA Ops:
  7.2 177.7 %all-gather.7.cloned.1.call-start = ((), (), s32[]{:S(2)}) async-start(), calls=%async_computation.6 | async-start | bytes 4587520 | tf_op jit(solution)/shard_map/all_gather | solution.py:41
  8.7 229.7 %copy-start.9 = (f32[64]{0:T(128)}, f32[64]{0:T(128)S(1)}, u32[]{:S(2)}) copy-start(f32[64]{0:T(128)S(1)} %add_rsqrt_fusion) | copy-start | bytes 772
  137.1 0.6 copy-start.5
  140.1 93.6 %all-gather.11.cloned.1.call-start = ((), (), s32[]{:S(2)}) async-start(), calls=%async_computation.8 | async-start | bytes 3784704 | tf_op jit(solution)/shard_map/all_gather | solution.py:31
  140.9 139.9 %all-gather.9.cloned.1.call-start = ((), (), s32[]{:S(2)}) async-start(), calls=%async_computation.7 | async-start | bytes 3784704 | tf_op jit(solution)/shard_map/all_gather | solution.py:32
  141.6 182.9 %all-gather.17.cloned.1.call-start = ((), (), s32[]{:S(2)}) async-start(), calls=%async_computation.12 | async-start | bytes 4587520 | tf_op jit(solution)/shard_map/all_gather | solution.py:64
  142.2 278.7 %all-gather.15.cloned.1.call-start = ((), (), s32[]{:S(2)}) async-start(), calls=%async_computation.10 | async-start | bytes 26492928 | tf_op jit(solution)/shard_map/all_gather | solution.py:33
  142.8 372.8 %all-gather.13.cloned.1.call-start = ((), (), s32[]{:S(2)}) async-start(), calls=%async_computation.9 | async-start | bytes 26492928 | tf_op jit(solution)/shard_map/all_gather | solution.py:30
  143.4 501.7 %reduce-scatter.9.cloned.1.call-start = ((), (), s32[]{:S(2)}) async-start(), calls=%async_computation.13 | async-start | bytes 4587520 | tf_op jit(solution)/shard_map/reduce_scatter | solution.py:81
  538.3 2.0 copy-start.4
  539.5 3.3 copy-start
  540.3 1.1 copy-start.7
  562.0 5.5 copy-start.1
  570.5 0.9 copy-start.8
  570.5 207.5 %reduce-scatter.7.cloned.1.call-start = ((), (), s32[]{:S(2)}) async-start(), calls=%async_computation.11 | async-start | bytes 4587520 | tf_op jit(solution)/shard_map/reduce_scatter | solution.py:61
  587.7 193.7 %reduce-scatter.15.cloned.1.call-start = ((), (), s32[]{:S(2)}) async-start(), calls=%async_computation.16 | async-start | bytes 7569408 | tf_op jit(solution)/shard_map/reduce_scatter | solution.py:95
  593.9 246.1 %reduce-scatter.13.cloned.1.call-start = ((), (), s32[]{:S(2)}) async-start(), calls=%async_computation.15 | async-start | bytes 7569408 | tf_op jit(solution)/shard_map/reduce_scatter | solution.py:94
  600.5 465.3 %reduce-scatter.11.cloned.1.call-start = ((), (), s32[]{:S(2)}) async-start(), calls=%async_computation.14 | async-start | bytes 52985856 | tf_op jit(solution)/shard_map/reduce_scatter | solution.py:93
  622.9 667.4 %reduce-scatter.17.cloned.1.call-start = ((), (), s32[]{:S(2)}) async-start(), calls=%async_computation.17 | async-start | bytes 52985856 | tf_op jit(solution)/shard_map/reduce_scatter | solution.py:96
  644.2 1.2 copy-start.2
  644.2 1.2 copy-start.6
  644.2 1.2 copy-start.10
  644.2 133.8 %copy-start.3 = (bf16[1,64,7168]{2,1,0:T(8,128)(2,1)S(1)}, bf16[1,64,7168]{2,1,0:T(8,128)(2,1)}, u32[]{:S(2)}) copy-start(bf16[1,64,7168]{2,1,0:T(8,128)(2,1)} %param.13) | copy-start | bytes 2752516
Sparse Core Ops, SparseCore 0:
  140.3 44.5 all-gather.6
  187.1 46.5 all-gather.10
  236.0 44.7 all-gather.8
  282.3 42.1 all-gather.16
  326.6 94.2 all-gather.14
  423.0 92.4 all-gather.12
  570.7 41.1 reduce-scatter.8
  614.2 42.2 reduce-scatter.6
  660.9 86.9 reduce-scatter.14
  752.1 87.8 reduce-scatter.12
  844.5 221.2 reduce-scatter.10
  1070.2 220.0 reduce-scatter.16
where the time goes:
time: 1310 us; the launch traced here: 1300 us
  waiting for transfers between devices  859 us (66%)
  blocking collectives  256 us (20%)
  matrix products  137 us (10%)
  between operations  16.4 us (1%)
  other arithmetic  15.4 us (1%)
    unnamed x2, blocking collectives  247 us
    reduce_scatter x1, waiting for transfers between devices, local_block(): lax.psum_scatter(grad_wq, 'dp', scatter_dimension=0, tiled=True)  226 us
    reduce_scatter x1, waiting for transfers between devices, local_block(): lax.psum_scatter(grad_wo, 'dp', scatter_dimension=1, tiled=True)  225 us
    all_gather x1, waiting for transfers between devices, local_block(): wo_full = lax.all_gather(w_out, 'dp', axis=1, tiled=True)  96.4 us
    all_gather x1, waiting for transfers between devices, local_block(): wq_full = lax.all_gather(w_query, 'dp', axis=0, tiled=True)  80.4 us
    reduce_scatter x1, waiting for transfers between devices, local_block(): lax.psum_scatter(grad_wk, 'dp', scatter_dimension=0, tiled=True)  58.5 us
    all_gather x1, waiting for transfers between devices, local_block(): wk_full = lax.all_gather(w_key, 'dp', axis=0, tiled=True)  48.8 us
    all_gather x1, waiting for transfers between devices, local_block(): wv_full = lax.all_gather(w_value, 'dp', axis=0, tiled=True)  42 us
  transfers between devices with their start and end apart: 12, of which 9 were waited for; matrix products, arithmetic and copies ran while one was open for 8% of the time, Pallas kernels for 0%

commit v1 on v0

v1 whole, which is shorter than its diff:
```python
import functools

import jax
import jax.numpy as jnp
from jax import lax
from jax.experimental import pallas as pl
from jax.experimental.pallas import tpu as pltpu
from jax.sharding import PartitionSpec as P

HEAD_DIM = 128
NORM_EPS = 1e-5
ROPE_BASE = 500000.0
SCORE_SCALE = HEAD_DIM ** -0.5
MASK_VALUE = -1e30
MESH = pl.DeviceIdType.MESH
ANY = pl.BlockSpec(memory_space=pl.ANY)
VMEM = pl.BlockSpec(memory_space=pltpu.VMEM)
F32, BF16 = jnp.float32, jnp.bfloat16

D = 7168
SEQ = 256
POS = 64
BLK = 448
HALF = 224
DZ = 1792
W_COLS = (640, 512, 384, 512)
Z_FIRST = (True, False, True, False)


class Place:
    def __init__(self):
        self.x = lax.axis_index("tp")
        dp = lax.axis_index("dp")
        self.z, self.y, self.c = dp // 8, (dp // 2) % 4, dp % 2

    def at(self, x=0, y=0, z=0, c=0):
        x, y, z = (self.x + x + 4) % 4, (self.y + y + 4) % 4, (self.z + z + 4) % 4
        return (x, (z * 4 + y) * 2 + (self.c + c) % 2)


def enter(place, offsets):
    barrier = pltpu.get_barrier_semaphore()
    for off in offsets:
        pl.semaphore_signal(barrier, inc=1, device_id=place.at(**off), device_id_type=MESH)
    pl.semaphore_wait(barrier, len(offsets))


def around(axis):
    return [{axis: 1}, {axis: -1}, {axis: 2}]


class Copies:
    def __init__(self, send, recv):
        self.send, self.recv, self.n, self.all = send, recv, 0, []

    def remote(self, src, dst, device):
        cp = pltpu.make_async_remote_copy(src, dst, self.send.at[self.n], self.recv.at[self.n], device_id=device, device_id_type=MESH)
        self.n += 1
        cp.start()
        self.all.append(cp)
        return cp

    def local(self, src, dst):
        cp = pltpu.make_async_copy(src, dst, self.send.at[self.n])
        self.n += 1
        cp.start()
        return cp

    def drain(self):
        for cp in self.all:
            cp.wait_send()


class Ring:
    def __init__(self, copies, place, axis, piece, own=None):
        self.copies, self.piece = copies, piece
        self.right, self.left = place.at(**{axis: 1}), place.at(**{axis: -1})
        self.own = own or (lambda h: piece(0, h))

    def start(self):
        c, p = self.copies, self.piece
        self.r0 = c.remote(self.own(0), p(0, 0), self.right)
        self.l0 = c.remote(self.own(1), p(0, 1), self.left)
        self.r1 = c.remote(self.own(1), p(0, 1), self.right)
        self.l1 = c.remote(self.own(0), p(0, 0), self.left)

    def forward(self):
        c, p = self.copies, self.piece
        self.r0.wait_recv()
        self.r2 = c.remote(p(-1, 0), p(-1, 0), self.right)
        self.l0.wait_recv()
        self.l2 = c.remote(p(1, 1), p(1, 1), self.left)

    def near(self):
        self.r1.wait_recv()
        self.l1.wait_recv()

    def far(self):
        self.r2.wait_recv()
        self.l2.wait_recv()


def params(cid, vmem=None):
    return pltpu.CompilerParams(collective_id=cid, has_side_effects=True, vmem_limit_bytes=vmem)


def gain_kernel(g_ref, o_ref, send, recv):
    me = Place()
    enter(me, [{"c": 1}] + around("y") + around("z"))
    cs = Copies(send, recv)
    o_ref[me.z, me.y, me.c] = g_ref[...]
    cs.remote(g_ref, o_ref.at[me.z, me.y, me.c], me.at(c=1)).wait_recv()
    for cp in [cs.remote(o_ref.at[me.z, me.y], o_ref.at[me.z, me.y], me.at(**off)) for off in around("y")]:
        cp.wait_recv()
    for cp in [cs.remote(o_ref.at[me.z], o_ref.at[me.z], me.at(**off)) for off in around("z")]:
        cp.wait_recv()
    cs.drain()


def gather_gain(norm_gain):
    padded = jnp.pad(norm_gain.astype(F32), (0, 1024 - HALF)).reshape(8, 128)
    out = pl.pallas_call(
        gain_kernel,
        out_shape=jax.ShapeDtypeStruct((4, 4, 2, 8, 128), F32),
        in_specs=[VMEM], out_specs=VMEM,
        scratch_shapes=[pltpu.SemaphoreType.DMA((7,)), pltpu.SemaphoreType.DMA((7,))],
        compiler_params=params(0), name="gather_gain",
    )(padded)
    return out.reshape(32, 1024)[:, :HALF].reshape(D)


def gather_kernel(*refs):
    w_in, (n_in, dy_in, n4_in, dy4_in) = refs[:4], refs[4:8]
    w_all, (n_all, dy_all, n4_all, dy4_all) = refs[8:12], refs[12:16]
    send, recv = refs[16:]
    me = Place()
    enter(me, [{"c": 1}] + around("x") + around("y") + around("z"))
    cs = Copies(send, recv)
    mate = me.at(c=1)

    rows = pl.ds(pl.multiple_of(me.c * HALF, HALF), HALF)
    first = []
    for w, buf in zip(w_in, w_all):
        first.append((cs.remote(w.at[1 - me.c], buf.at[me.z, me.y, rows], mate), cs.local(w.at[me.c], buf.at[me.z, me.y, rows])))

    def x_piece(buf):
        return lambda off, h: buf.at[me.c, (me.x + off + 4) % 4, pl.ds(h * 32, 32)]

    def x_ring(buf, src):
        return Ring(cs, me, "x", x_piece(buf), lambda h: src.at[pl.ds(h * 32, 32)])

    def x4_ring(buf):
        return Ring(cs, me, "x", lambda off, h: buf.at[pl.ds(2 * h, 2), me.c, (me.x + off + 4) % 4])

    acts = []
    for buf, src in ((n_all, n_in), (dy_all, dy_in)):
        ring = x_ring(buf, src)
        ring.start()
        acts.append((ring, cs.local(src, buf.at[me.c, me.x]), buf))
    fours = []
    for buf, src, axis in ((n4_all, n4_in, "z"), (dy4_all, dy4_in, "y")):
        here = getattr(me, axis)
        moves = [cs.remote(src.at[(here + off[axis] + 4) % 4], buf.at[here, me.c, me.x], me.at(**off)) for off in around(axis)]
        fours.append((moves, cs.local(src.at[here], buf.at[here, me.c, me.x]), x4_ring(buf), buf))

    def phase1(buf, z_first):
        if z_first:
            return Ring(cs, me, "z", lambda off, h: buf.at[(me.z + off + 4) % 4, me.y, pl.ds(h * HALF, HALF)])
        return Ring(cs, me, "y", lambda off, h: buf.at[me.z, (me.y + off + 4) % 4, pl.ds(h * HALF, HALF)])

    def phase2(buf, z_first):
        if z_first:
            return Ring(cs, me, "y", lambda off, h: buf.at[pl.ds(2 * h, 2), (me.y + off + 4) % 4])
        return Ring(cs, me, "z", lambda off, h: buf.at[(me.z + off + 4) % 4, pl.ds(2 * h, 2)])

    ones = [phase1(b, f) for b, f in zip(w_all, Z_FIRST)]
    twos = [phase2(b, f) for b, f in zip(w_all, Z_FIRST)]
    for (remote, local), ring in zip(first, ones):
        remote.wait_recv()
        local.wait()
        ring.start()
    for ring in ones:
        ring.forward()
    for one, two in zip(ones[:2], twos[:2]):
        one.near()
        one.far()
        two.start()
    for one, two in zip(ones[2:], twos[2:]):
        one.near()
        one.far()
        two.start()
    for ring, local, buf in acts:
        local.wait()
        ring.forward()
        ring.near()
    for moves, local, ring, buf in fours:
        for cp in moves:
            cp.wait_recv()
        local.wait()
        ring.start()
    tail = []
    for ring, local, buf in acts:
        for k in (0, 1, -1):
            p = buf.at[me.c, (me.x + k + 4) % 4]
            tail.append(cs.remote(p, p, mate))
    for ring in twos[:2]:
        ring.forward()
    for ring, local, buf in acts:
        ring.far()
        p = buf.at[me.c, (me.x + 2) % 4]
        tail.append(cs.remote(p, p, mate))
    for moves, local, ring, buf in fours:
        ring.forward()
        ring.near()
        for k in (0, 1, -1):
            p = buf.at[:, me.c, (me.x + k + 4) % 4]
            tail.append(cs.remote(p, p, mate))
    for ring in twos[2:]:
        ring.forward()
    for moves, local, ring, buf in fours:
        ring.far()
        p = buf.at[:, me.c, (me.x + 2) % 4]
        tail.append(cs.remote(p, p, mate))
    for ring in twos:
        ring.near()
        ring.far()
    for cp in tail:
        cp.wait_recv()
    cs.drain()


def gather_all(w_in, normed, grad_out, normed4, grad4):
    n_cp = 4 * 14 + 2 * 7 + 2 * 10 + 16
    shapes = [jax.ShapeDtypeStruct((4, 4, BLK, cols), BF16) for cols in W_COLS]
    shapes += [jax.ShapeDtypeStruct((2, 4, POS, D), BF16)] * 2
    shapes += [jax.ShapeDtypeStruct((4, 2, 4, POS, DZ), BF16)] * 2
    return pl.pallas_call(
        gather_kernel,
        out_shape=shapes,
        in_specs=[VMEM] * 8, out_specs=[ANY] * 8,
        scratch_shapes=[pltpu.SemaphoreType.DMA((n_cp,)), pltpu.SemaphoreType.DMA((n_cp,))],
        compiler_params=params(1), name="gather_all",
    )(*w_in, normed, grad_out, normed4, grad4)


def exchange_kernel(o_in, dn_in, a_in, g_in, o_out, dn_out, a_all, g_all, mine, got, parts, res, send, recv):
    me = Place()
    enter(me, [{"c": 1}] + around("x") + around("y") + around("z"))
    cs = Copies(send, recv)
    mate = me.at(c=1)
    swaps = []
    for t, src in enumerate((o_in, dn_in)):
        swaps.append((cs.remote(src.at[1 - me.c], got.at[t], mate), cs.local(src.at[me.c], mine.at[t])))
    rings = []
    for src, buf, axis in ((a_in, a_all, "y"), (g_in, g_all, "z")):
        here = getattr(me, axis)

        def piece(off, h, buf=buf, here=here):
            return buf.at[(here + off + 4) % 4, pl.ds(h * 256, 256)]

        ring = Ring(cs, me, axis, piece, lambda h, src=src: src.at[pl.ds(h * 256, 256)])
        ring.start()
        rings.append((ring, cs.local(src, buf.at[here])))
    sends = []
    for t in range(2):
        swaps[t][0].wait_recv()
        swaps[t][1].wait()
        for k, off in ((2, 2), (0, 1), (1, -1), (3, 0)):
            blk = (me.x + off + 4) % 4

            @pl.loop(0, POS // 16)
            def _(i):
                r = pl.ds(pl.multiple_of(i * 16, 16), 16)
                s = mine[t, blk, r, :].astype(F32) + got[t, blk, r, :].astype(F32)
                mine[t, blk, r, :] = s.astype(BF16)

            if off:
                sends.append(cs.remote(mine.at[t, blk], parts.at[t, k], me.at(x=off)))
    for ring, local in rings:
        ring.forward()
    for t, dst in enumerate((o_out, dn_out)):
        for cp in sends[3 * t:3 * t + 3]:
            cp.wait_recv()

        @pl.loop(0, POS // 16)
        def _(i):
            r = pl.ds(pl.multiple_of(i * 16, 16), 16)
            s = mine[t, me.x, r, :].astype(F32) + parts[t, 0, r, :].astype(F32)
            s = s + parts[t, 1, r, :].astype(F32) + parts[t, 2, r, :].astype(F32)
            dst[r, :] = s.astype(BF16)

    for ring, local in rings:
        ring.near()
        ring.far()
        local.wait()
    cs.drain()


def exchange(o_part, dn_part, attn, grad_qkv):
    ca, cg = attn.shape[1], grad_qkv.shape[1]
    return pl.pallas_call(
        exchange_kernel,
        out_shape=[jax.ShapeDtypeStruct((POS, D), BF16)] * 2
        + [jax.ShapeDtypeStruct((4, 512, ca), BF16), jax.ShapeDtypeStruct((4, 512, cg), BF16)],
        in_specs=[ANY] * 4, out_specs=[VMEM, VMEM, ANY, ANY],
        scratch_shapes=[pltpu.VMEM((2, 4, POS, D), BF16), pltpu.VMEM((2, 4, POS, D), BF16), pltpu.VMEM((2, 3, POS, D), BF16),
                        pltpu.VMEM((8, 128), F32),
                        pltpu.SemaphoreType.DMA((24,)), pltpu.SemaphoreType.DMA((24,))],
        compiler_params=params(2, 60 * 2**20), name="exchange",
    )(o_part, dn_part, attn, grad_qkv)


def scatter_kernel(q_in, o_in, q_out, o_out, send, recv):
    me = Place()
    enter(me, [{axis: k, "c": c} for axis in ("y", "z") for k in (1, -1, 2) for c in (0, 1)] + [{"c": 1}])
    cs = Copies(send, recv)
    waits, locals_ = [], []
    for k, off in ((3, 2), (1, 1), (2, -1), (0, 0)):
        for dc in (0, 1):
            for src, dst, axis in ((q_in, q_out, "y"), (o_in, o_out, "z")):
                blk = (getattr(me, axis) + off + 4) % 4
                core = (me.c + dc) % 2
                piece, slot = src.at[blk, core], dst.at[k, me.c]
                if off or dc:
                    waits.append(cs.remote(piece, slot, me.at(**{axis: off, "c": dc})))
                else:
                    locals_.append(cs.local(piece, slot))
    for cp in waits:
        cp.wait_recv()
    for cp in locals_:
        cp.wait()
    cs.drain()


def scatter(grad_q, grad_o):
    cq, co = grad_q.shape[-1], grad_o.shape[-1]
    return pl.pallas_call(
        scatter_kernel,
        out_shape=[jax.ShapeDtypeStruct((4, 2, HALF, cq), F32), jax.ShapeDtypeStruct((4, 2, HALF, co), F32)],
        in_specs=[ANY] * 2, out_specs=[ANY] * 2,
        scratch_shapes=[pltpu.SemaphoreType.DMA((16,)), pltpu.SemaphoreType.DMA((16,))],
        compiler_params=params(3), name="scatter",
    )(grad_q, grad_o)


def gain_grad_kernel(p_ref, o_ref, rz, ry, rc, rx, sz, sy, sc, sx, send, recv):
    me = Place()
    enter(me, [{"c": 1}] + around("x") + around("y") + around("z"))
    cs = Copies(send, recv)

    def stage(src, slots, axis):
        here = getattr(me, axis)
        offs = [{"c": 1}] if axis == "c" else around(axis)
        n = 2 if axis == "c" else 4
        sent = [cs.remote(src((here + off[axis] + n) % n), slots.at[here], me.at(**off)) for off in offs]
        slots[here] = src(here)[...]
        for cp in sent:
            cp.wait_recv()
        total = slots[0]
        for k in range(1, n):
            total = total + slots[k]
        return total

    sz[...] = stage(lambda k: p_ref.at[k], rz, "z")
    sy[...] = stage(lambda k: sz.at[k], ry, "y")
    sc[...] = stage(lambda k: sy.at[k], rc, "c")
    o_ref[...] = stage(lambda k: sc, rx, "x")
    cs.drain()


def reduce_gain(part):
    padded = jnp.pad(part.reshape(32, HALF), ((0, 0), (0, 1024 - HALF))).reshape(4, 4, 2, 8, 128)
    out = pl.pallas_call(
        gain_grad_kernel,
        out_shape=jax.ShapeDtypeStruct((8, 128), F32),
        in_specs=[VMEM], out_specs=VMEM,
        scratch_shapes=[pltpu.VMEM((4, 4, 2, 8, 128), F32), pltpu.VMEM((4, 2, 8, 128), F32), pltpu.VMEM((2, 8, 128), F32), pltpu.VMEM((4, 8, 128), F32),
                        pltpu.VMEM((4, 2, 8, 128), F32), pltpu.VMEM((2, 8, 128), F32), pltpu.VMEM((8, 128), F32), pltpu.VMEM((8, 128), F32),
                        pltpu.SemaphoreType.DMA((10,)), pltpu.SemaphoreType.DMA((10,))],
        compiler_params=params(4), name="reduce_gain",
    )(padded)
    return out.reshape(1024)[:HALF]


def rope_tables(seq_len):
    half_dim = HEAD_DIM // 2
    inv_freq = ROPE_BASE ** (-jnp.arange(half_dim, dtype=F32) * 2.0 / HEAD_DIM)
    angles = jnp.arange(seq_len, dtype=F32)[:, None] * inv_freq[None, :]
    return jnp.cos(angles), jnp.sin(angles)


def rotate(values, cos_t, sin_t):
    half_dim = values.shape[-1] // 2
    lower_half = values[..., :half_dim]
    upper_half = values[..., half_dim:]
    return jnp.concatenate([lower_half * cos_t - upper_half * sin_t, upper_half * cos_t + lower_half * sin_t], axis=-1)


def dot(spec, a, b):
    return jnp.einsum(spec, a, b, preferred_element_type=F32)


def solution(mesh):
    def local_block(hidden, norm_gain, w_query, w_key, w_value, w_out, grad_out):
        gain_full = gather_gain(norm_gain)
        hidden, grad_out = hidden[0], grad_out[0]
        hidden_f32 = hidden.astype(F32)
        inv_rms = lax.rsqrt(jnp.mean(hidden_f32 * hidden_f32, axis=-1, keepdims=True) + NORM_EPS)
        x_hat = hidden_f32 * inv_rms
        normed = (x_hat * gain_full).astype(BF16)

        w_out_t = w_out.T
        q2 = w_query.reshape(HALF, 2, 896)
        o2 = w_out_t.reshape(HALF, 2, 896)
        k2, v2 = w_key.reshape(HALF, 2, 128), w_value.reshape(HALF, 2, 128)
        w_in = [q2[:, :, :640], jnp.concatenate([q2[:, :, 640:], k2, v2], -1), o2[:, :, :384], o2[:, :, 384:]]
        w_in = [jnp.moveaxis(w, 1, 0) for w in w_in]
        n4 = jnp.moveaxis(normed.reshape(POS, 4, DZ), 1, 0)
        dy4 = jnp.moveaxis(grad_out.reshape(POS, 4, 4, BLK), 2, 0).reshape(4, POS, DZ)
        *w_all, n_all, dy_all, n4_all, dy4_all = gather_all(w_in, normed, grad_out, n4, dy4)
        w0, w1, w2, w3 = [w.reshape(D, -1) for w in w_all]
        n_all, dy_all = n_all.reshape(512, D), dy_all.reshape(512, D)
        n4_all, dy4_all = n4_all.reshape(2048, DZ), dy4_all.reshape(2048, DZ)

        cos_t, sin_t = rope_tables(SEQ)
        cos_q, sin_q = cos_t[:, None, :], sin_t[:, None, :]
        qa = dot("td,de->te", n_all, w0).astype(BF16)
        qb = dot("td,de->te", n_all, w1).astype(BF16)
        q_lin = jnp.concatenate([qa, qb[:, :256]], -1).reshape(2, SEQ, 7, HEAD_DIM)
        k_lin, v_heads = qb[:, 256:384].reshape(2, SEQ, HEAD_DIM), qb[:, 384:].reshape(2, SEQ, HEAD_DIM)
        q_heads = rotate(q_lin.astype(F32), cos_q, sin_q).astype(BF16)
        k_heads = rotate(k_lin.astype(F32), cos_t, sin_t).astype(BF16)
        causal = jnp.arange(SEQ)[:, None] >= jnp.arange(SEQ)[None, :]
        scores = dot("bqrd,bkd->brqk", q_heads, k_heads) * SCORE_SCALE
        attn_prob = jax.nn.softmax(jnp.where(causal, scores, MASK_VALUE), axis=-1)
        prob_bf16 = attn_prob.astype(BF16)
        attn = dot("brqk,bkd->bqrd", prob_bf16, v_heads).astype(BF16).reshape(512, 896)
        o_part = (dot("te,de->td", attn[:, :384], w2) + dot("te,de->td", attn[:, 384:], w3)).astype(BF16)

        ga = [dot("td,de->te", dy_all, w).astype(BF16) for w in (w2, w3)]
        grad_attn = jnp.concatenate(ga, -1).reshape(2, SEQ, 7, HEAD_DIM)
        grad_v = dot("brqk,bqrd->bkd", prob_bf16, grad_attn).astype(BF16)
        grad_prob = dot("bqrd,bkd->brqk", grad_attn, v_heads)
        grad_scores = attn_prob * (grad_prob - jnp.sum(grad_prob * attn_prob, axis=-1, keepdims=True))
        grad_scores = (grad_scores * SCORE_SCALE).astype(BF16)
        grad_q = dot("brqk,bkd->bqrd", grad_scores, k_heads).astype(BF16)
        grad_k = dot("brqk,bqrd->bkd", grad_scores, q_heads).astype(BF16)
        gq = rotate(grad_q.astype(F32), cos_q, -sin_q).astype(BF16).reshape(512, 896)
        gk = rotate(grad_k.astype(F32), cos_t, -sin_t).astype(BF16).reshape(512, 128)
        gqkv = jnp.concatenate([gq, gk, grad_v.reshape(512, 128)], -1)
        dn_part = (dot("te,de->td", gqkv[:, :640], w0) + dot("te,de->td", gqkv[:, 640:], w1)).astype(BF16)

        o_sum, dn_sum, attn_all, gqkv_all = exchange(o_part.reshape(2, 4, POS, D), dn_part.reshape(2, 4, POS, D), attn, gqkv)
        hidden_out = (hidden_f32 + o_sum.astype(F32)).astype(BF16)
        grad_normed = dn_sum.astype(F32)
        value_a9 = grad_normed * gain_full
        grad_hidden = (grad_out.astype(F32) + inv_rms * (value_a9 - x_hat * jnp.mean(value_a9 * x_hat, axis=-1, keepdims=True))).astype(BF16)
        grad_gain = reduce_gain(jnp.sum(grad_normed * x_hat, axis=0))

        gw = dot("td,te->de", n4_all, gqkv_all.reshape(2048, 1152)).reshape(4, 2, HALF, 1152)
        gwo = dot("td,te->de", dy4_all, attn_all.reshape(2048, 896)).reshape(4, 2, HALF, 896)
        gw, gwo = scatter(gw, gwo)
        gw, gwo = jnp.sum(gw, 0), jnp.sum(gwo, 0)
        gw = jnp.moveaxis(gw, 0, 1)
        grad_wo = jnp.moveaxis(gwo, 0, 1).reshape(HALF, DZ).T
        return (
            hidden_out[None],
            grad_hidden[None],
            grad_gain,
            gw[:, :, :896].reshape(HALF, DZ),
            gw[:, :, 896:1024].reshape(HALF, 256),
            gw[:, :, 1024:].reshape(HALF, 256),
            grad_wo,
        )

    act_spec = P("dp", "tp", None)
    col_spec = P("dp", "tp")
    row_spec = P("tp", "dp")
    return jax.shard_map(
        local_block,
        mesh=mesh,
        in_specs=(act_spec, P("dp"), col_spec, col_spec, col_spec, row_spec, act_spec),
        out_specs=(act_spec, act_spec, P("dp"), col_spec, col_spec, col_spec, row_spec),
        check_vma=False,
    )
```

time: 1310 us -> 609 us (0.46)
  waiting for transfers between devices: 859 us -> 0 us
  Pallas kernels: 0 us -> 380 us
  blocking collectives: 256 us -> 0 us
  local copies, waits for them, and re-layouts: 12.8 us -> 60.4 us
  between operations: 16.4 us -> 1.28 us
  other arithmetic: 15.4 us -> 29 us
    reduce_scatter x6 -> x0, waiting for transfers between devices: 509 us -> none  [the longest x1 226 us: local_block(): lax.psum_scatter(grad_wq, 'dp', scatter_dimension=0, tiled=True)]
    pallas_call x0 -> x5, Pallas kernels: none -> 380 us  [the longest x1 166 us: gather_all(): pl.pallas_call(gather_kernel, out_shape=shapes, in_specs=[VMEM] * 8, out_...]
    all_gather x6 -> x0, waiting for transfers between devices: 347 us -> none  [the longest x1 96.4 us: local_block(): wo_full = lax.all_gather(w_out, 'dp', axis=1, tiled=True)]
    unnamed x2 -> x0, blocking collectives: 247 us -> none
    dot_general x0 -> x2, local copies, waits for them, and re-layouts: none -> 21.1 us  [dot(): return jnp.einsum(spec, a, b, preferred_element_type=F32)]
    reshape x0 -> x12, local copies, waits for them, and re-layouts: none -> 17 us  [the longest x1 2.69 us: local_block(): grad_wo = jnp.moveaxis(gwo, 0, 1).reshape(HALF, DZ).T]
    dot_general x18 -> x15, matrix products: 137 us -> 129 us  [dot(): return jnp.einsum(spec, a, b, preferred_element_type=F32)]
  transfers between devices with their start and end apart: 12 -> 0, of which waited for: 9 -> 0; matrix products, arithmetic and copies ran while one was open for 8% -> 0% of each run, Pallas kernels for 0% -> 0%
where the time goes in v1:
time: 609 us; the launch traced here: 605 us
  Pallas kernels  380 us (62%)
  matrix products  135 us (22%)
  local copies, waits for them, and re-layouts  60.4 us (10%)
  other arithmetic  29 us (5%)
    pallas_call x1, Pallas kernels, gather_all(): pl.pallas_call(gather_kernel, out_shape=shapes, in_specs=[VMEM] * 8, out_...  166 us
    dot_general x15, matrix products, dot(): return jnp.einsum(spec, a, b, preferred_element_type=F32)  129 us
    pallas_call x1, Pallas kernels, scatter(): pl.pallas_call(scatter_kernel, out_shape=[jax.ShapeDtypeStruct((4, 2, HAL...  92.7 us
    pallas_call x1, Pallas kernels, exchange(): pl.pallas_call(exchange_kernel, out_shape=[jax.ShapeDtypeStruct((POS, D),...  91.5 us
    dot_general x2, local copies, waits for them, and re-layouts, dot(): return jnp.einsum(spec, a, b, preferred_element_type=F32)  21.1 us
    pallas_call x1, Pallas kernels, gather_gain(): pl.pallas_call(gain_kernel, out_shape=jax.ShapeDtypeStruct((4, 4, 2, 8, 1...  14.7 us
    pallas_call x1, Pallas kernels, reduce_gain(): pl.pallas_call(gain_grad_kernel, out_shape=jax.ShapeDtypeStruct((8, 128),...  14.5 us

profile of v1, /device:TPU:1, one launch (start us, length us, event | category | flops | bytes accessed | tf_op | source)
XLA Modules:
  0.0 604.9 jit_solution(10941847518999275478)
XLA Ops:
  4.1 14.7 %gather_gain.1 = f32[4,4,2,8,128]{4,3,2,1,0:T(8,128)} custom-call(f32[8,128]{1,0:T(8,128)} %bitcast_convert_fusion.g_ref), custom_call_target="tpu_custom_call" | custom-call | tf_op jit(solution)/shard_map/gather_gain/pallas_call | solution.py:122
  38.4 166.4 %gather_all.1 = (bf16[4,4,448,640]{3,2,1,0:T(8,128)(2,1)}, bf16[4,4,448,512]{3,2,1,0:T(8,128)(2,1)}, bf16[4,4,448,384]{3,2,1,0:T(8,128)(2,1)}, bf16[4,4,448,512]...) custom-call(bf16[2,224,640]{2,1,0:T(8,128)(2,1)} %bitcast.262, ...), custom_call_target="tpu_custom_call" | custom-call | tf_op jit(solution)/shard_map/gather_all/pallas_call | solution.py:237
  204.8 7.8 %convolution_convert_fusion.4 = bf16[512,384]{0,1:T(8,128)(2,1)S(1)} fusion(bf16[512,7168]{1,0:T(8,128)(2,1)} %bitcast.284, bf16[7168,384]{1,0:T(8,128)(2,1)} %bitcast.255), kind=kOutput, calls=%fused_computation.49 | convolution fusion | flops 2818768896 | bytes 13238272 | tf_op jit(solution)/shard_map/td,de->te/dot_general | solution.py:400
  212.7 6.5 %convolution_convert_fusion.2 = bf16[512,512]{0,1:T(8,128)(2,1)S(1)} fusion(bf16[512,7168]{1,0:T(8,128)(2,1)} %bitcast.285, bf16[7168,512]{1,0:T(8,128)(2,1)S(1)} %bitcast.253), kind=kOutput, calls=%fused_computation.47 | convolution fusion | flops 3758358528 | bytes 15204352 | tf_op jit(solution)/shard_map/td,de->te/dot_general | solution.py:400
  221.7 9.1 %convolution_convert_fusion.3 = bf16[512,512]{1,0:T(8,128)(2,1)S(1)} fusion(bf16[512,7168]{1,0:T(8,128)(2,1)} %bitcast.282, bf16[7168,512]{1,0:T(8,128)(2,1)} %bitcast.246), kind=kOutput, calls=%fused_computation.48 | convolution fusion | flops 3758358528 | bytes 15204352 | tf_op jit(solution)/shard_map/td,de->te/dot_general | solution.py:400
  230.9 10.8 %convolution_convert_fusion.1 = bf16[512,640]{1,0:T(8,128)(2,1)S(1)} fusion(bf16[512,7168]{1,0:T(8,128)(2,1)} %bitcast.283, bf16[7168,640]{1,0:T(8,128)(2,1)} %bitcast.280), kind=kOutput, calls=%fused_computation.45 | convolution fusion | flops 4697948160 | bytes 17170432 | tf_op jit(solution)/shard_map/td,de->te/dot_general | solution.py:400
  248.6 5.0 fusion.53
  253.6 3.5 fusion.26
  262.7 7.4 %fusion.28 = f32[2,256,128]{2,1,0:T(8,128)S(1)} fusion(f32[2,256,256,7]{2,1,3,0:T(8,128)} %fusion.54, bf16[2,256,7,64]{3,1,2,0:T(8,128)(2,1)} %get-tuple-element.38, bf16[2,256,7,64]{3,1,2,0:T(8,128)(2,1)} %copy-done.9, f32[2,7,256,256]{2,3,1,0:T(8,128)} %get-tuple-element.57, f32[2,7,256]{2,1,0:T(8,128)S(1)} %get-tuple-element.56), kind=kOutput, calls=%fused_computation.54 | convolution fusion | flops 243273472 | bytes 8534016 | tf_op jit(solution)/shard_map/brqk,bqrd->bkd/dot_general | solution.py:400
  270.1 8.1 %convert_bitcast_fusion = f32[2,256,7,128]{3,1,2,0:T(8,128)} fusion(f32[2,256,256,7]{2,1,3,0:T(8,128)} %fusion.54, bf16[2,256,64]{2,1,0:T(8,128)(2,1)S(1)} %copy-done.15, bf16[2,256,64]{2,1,0:T(8,128)(2,1)S(1)} %copy-done.13, f32[2,7,256,256]{2,3,1,0:T(8,128)} %get-tuple-element.57, f32[2,7,256]{2,1,0:T(8,128)S(1)} %get-tuple-element.56), kind=kOutput, calls=%fused_computation.29 | convolution fusion | flops 242487040 | bytes 9320448 | tf_op jit(solution)/shard_map/brqk,bkd->bqrd/dot_general | solution.py:400
  290.4 12.0 %fusion.34 = f32[512,7168]{1,0:T(8,128)} fusion(bf16[7168,640]{1,0:T(8,128)(2,1)} %bitcast.281, bf16[512,896]{0,1:T(8,128)(2,1)} %bitcast.259), kind=kOutput, calls=%fused_computation.65 | convolution fusion | flops 4697620480 | bytes 24510464 | tf_op jit(solution)/shard_map/te,de->td/dot_general | solution.py:400
  302.4 11.5 %add_convert_fusion = bf16[512,7168]{1,0:T(8,128)(2,1)} fusion(f32[512,7168]{1,0:T(8,128)} %fusion.34, bf16[7168,512]{1,0:T(8,128)(2,1)} %bitcast.247, bf16[512,1152]{1,0:T(8,128)(2,1)S(1)} %concatenate.40.g_in), kind=kOutput, calls=%fused_computation.2 | convolution fusion | flops 3765436416 | bytes 29884416 | tf_op jit(solution)/shard_map/te,de->td/dot_general | solution.py:400
  313.9 10.8 %fusion.37 = f32[512,7168]{1,0:T(8,128)} fusion(bf16[7168,512]{1,0:T(8,128)(2,1)} %bitcast.252, bf16[512,896]{0,1:T(8,128)(2,1)S(1)} %bitcast.241), kind=kOutput, calls=%fused_computation.69 | convolution fusion | flops 3758096384 | bytes 22544384 | tf_op jit(solution)/shard_map/te,de->td/dot_general | solution.py:400
  324.7 10.8 %add_convert_fusion.1 = bf16[512,7168]{1,0:T(8,128)(2,1)} fusion(f32[512,7168]{1,0:T(8,128)} %fusion.37, bf16[7168,384]{1,0:T(8,128)(2,1)} %bitcast.256, bf16[512,896]{0,1:T(8,128)(2,1)S(1)} %bitcast.242), kind=kOutput, calls=%fused_computation.3 | convolution fusion | flops 2825912320 | bytes 27918336 | tf_op jit(solution)/shard_map/te,de->td/dot_general | solution.py:400
  335.5 91.5 %exchange.1 = (bf16[64,7168]{1,0:T(8,128)(2,1)}, bf16[64,7168]{1,0:T(8,128)(2,1)}, bf16[4,512,896]{2,1,0:T(8,128)(2,1)}, bf16[4,512,1152]{2,1,0:T(8,128)(2,1)}) custom-call(bf16[2,4,64,7168]{3,2,1,0:T(8,128)(2,1)} %bitcast.238, bf16[2,4,64,7168]{3,2,1,0:T(8,128)(2,1)} %bitcast.239, bf16[512,896]{1,0:T(8,128)(2,1)} %copy.110.a_in, bf16[512,1152]{1,0:T(8,128)(2,1)} %copy-done.6), custom_call_target="tpu_custom_call" | custom-call | tf_op jit(solution)/shard_map/exchange/pallas_call | solution.py:301
  428.9 3.4 fusion.31
  433.1 14.5 %reduce_gain.1 = f32[8,128]{1,0:T(8,128)} custom-call(f32[4,4,2,8,128]{4,3,2,1,0:T(8,128)} %bitcast.272), custom_call_target="tpu_custom_call" | custom-call | tf_op jit(solution)/shard_map/reduce_gain/pallas_call | solution.py:373
  448.8 10.5 %copy.111 = bf16[1792,2048]{1,0:T(8,128)(2,1)} copy(bf16[1792,2048]{0,1:T(8,128)(2,1)} %bitcast.249) | data formatting | bytes 14680064 | tf_op jit(solution)/shard_map/td,te->de/dot_general | solution.py:400
  459.4 15.2 %fusion.55.q_in = f32[4,2,224,1152]{3,2,1,0:T(8,128)} fusion(bf16[4,2,224,2048]{3,2,1,0:T(8,128)(2,1)} %bitcast.250, bf16[2048,1152,1,1]{1,0,3,2:T(8,128)(2,1)} %bitcast.286), kind=kOutput, calls=%fused_computation.108 | convolution fusion | flops 8455716864 | bytes 20316160 | tf_op jit(solution)/shard_map/td,te->de/dot_general | solution.py:400
  474.6 10.5 %copy.112 = bf16[1792,2048]{1,0:T(8,128)(2,1)} copy(bf16[1792,2048]{0,1:T(8,128)(2,1)} %bitcast.248) | data formatting | bytes 14680064 | tf_op jit(solution)/shard_map/td,te->de/dot_general | solution.py:400
  485.1 12.9 %fusion.56.o_in = f32[4,2,224,896]{3,2,1,0:T(8,128)} fusion(bf16[4,2,224,2048]{3,2,1,0:T(8,128)(2,1)} %bitcast.251, bf16[2048,896,1,1]{1,0,3,2:T(8,128)(2,1)} %bitcast.287), kind=kOutput, calls=%fused_computation.109 | convolution fusion | flops 6576668672 | bytes 17432576 | tf_op jit(solution)/shard_map/td,te->de/dot_general | solution.py:400
  498.0 92.7 %scatter.1 = (f32[4,2,224,1152]{3,2,1,0:T(8,128)}, f32[4,2,224,896]{3,2,1,0:T(8,128)}) custom-call(f32[4,2,224,1152]{3,2,1,0:T(8,128)} %fusion.55.q_in, f32[4,2,224,896]{3,2,1,0:T(8,128)} %fusion.56.o_in), custom_call_target="tpu_custom_call" | custom-call | tf_op jit(solution)/shard_map/scatter/pallas_call | solution.py:337
  590.7 4.0 reduce_sum.68
  594.7 4.5 reduce_sum.69
  (101 shorter events, 59.4 us)
Async XLA Ops:
  0.6 19.9 %copy-start = (bf16[224,256]{1,0:T(8,128)(2,1)S(1)}, bf16[224,256]{1,0:T(8,128)(2,1)}, u32[]{:S(2)}) copy-start(bf16[224,256]{1,0:T(8,128)(2,1)} %param.10) | copy-start | bytes 344068
  24.7 6.5 %copy-start.2 = (bf16[1,64,7168]{2,1,0:T(8,128)(2,1)S(1)}, bf16[1,64,7168]{2,1,0:T(8,128)(2,1)}, u32[]{:S(2)}) copy-start(bf16[1,64,7168]{2,1,0:T(8,128)(2,1)} %param.7) | copy-start | bytes 2752516
  25.6 6.8 %copy-start.3 = (bf16[1,64,7168]{2,1,0:T(8,128)(2,1)S(1)}, bf16[1,64,7168]{2,1,0:T(8,128)(2,1)}, u32[]{:S(2)}) copy-start(bf16[1,64,7168]{2,1,0:T(8,128)(2,1)} %param.13) | copy-start | bytes 2752516
  33.8 3.3 copy-start.16
  204.8 7.9 %copy-start.5 = (bf16[4,4,448,512]{3,2,1,0:T(8,128)(2,1)S(1)}, bf16[4,4,448,512]{3,2,1,0:T(8,128)(2,1)}, u32[]{:S(2)}) copy-start(bf16[4,4,448,512]{3,2,1,0:T(8,128)(2,1)} %get-tuple-element.25) | copy-start | bytes 22020100
  246.9 1.7 copy-start.13
  246.9 1.7 copy-start.14
  246.9 1.7 copy-start.17
  248.5 5.0 copy-start.9
  248.5 5.0 copy-start.7
  253.6 3.5 copy-start.10
  253.6 3.5 copy-start.18
  262.7 7.4 %copy-start.15 = (bf16[2,256,64]{2,1,0:T(8,128)(2,1)S(1)}, bf16[2,256,64]{2,1,0:T(8,128)(2,1)}, u32[]{:S(2)}) copy-start(bf16[2,256,64]{2,1,0:T(8,128)(2,1)} %get-tuple-element.50) | copy-start | bytes 196612
  281.8 6.2 %copy-start.11 = (bf16[2,256,64]{2,1,0:T(8,128)(2,1)S(1)}, bf16[2,256,64]{2,1,0:T(8,128)(2,1)}, u32[]{:S(2)}) copy-start(bf16[2,256,64]{2,1,0:T(8,128)(2,1)} %get-tuple-element.48) | copy-start | bytes 196612
  281.8 6.2 %copy-start.12 = (bf16[2,256,128]{2,1,0:T(8,128)(2,1)S(1)}, bf16[2,256,128]{2,1,0:T(8,128)(2,1)}, u32[]{:S(2)}) copy-start(bf16[2,256,128]{2,1,0:T(8,128)(2,1)} %fusion.26) | copy-start | bytes 393220
  285.8 0.9 copy-start.8
  290.4 12.0 %copy-start.6 = (bf16[512,1152]{1,0:T(8,128)(2,1)}, bf16[512,1152]{1,0:T(8,128)(2,1)S(1)}, u32[]{:S(2)}) copy-start(bf16[512,1152]{1,0:T(8,128)(2,1)S(1)} %concatenate.40.g_in) | copy-start | bytes 3538948
  335.5 93.4 %copy-start.4 = (bf16[1,64,7168]{2,1,0:T(8,128)(2,1)S(1)}, bf16[1,64,7168]{2,1,0:T(8,128)(2,1)}, u32[]{:S(2)}) copy-start(bf16[1,64,7168]{2,1,0:T(8,128)(2,1)} %param.13) | copy-start | bytes 2752516
  601.9 2.8 copy-start.1
